TPU v7x, 32 devices: a whole 2x2x4 slice. The times are simulated.
32 devices in a mesh: period: 2 (over y), gx: 4 (over z), gy: 2 (over x), gz: 2 (over core).
Axes of the slice: x: 2, y: 2, z: 4, core: 2. Of those that a mesh axis runs over, the one named last changes fastest.
Arguments:
- residual: float32 [4, 3, 16, 16, 256], P('period', None, 'gx', 'gy', 'gz'), parts along dimension 0, may hold values from -6 to 6
- classes: int32 [16, 16, 256], P('gx', 'gy', 'gz'), may hold values from 0 to 15
- edge_mask: int32 [3, 16, 16, 256], P(None, 'gx', 'gy', 'gz'), may hold values from 0 to 1
- class_weight: float32 [32], P('period'), parts along dimension 0, may hold values from 0.01 to 1
Outputs:
- preconditioned: float32 [4, 3, 16, 16, 256], P('period', None, 'gx', 'gy', 'gz'), parts along dimension 0
There are 2 independent parts, one for each index of `period`. A program takes and returns all parts, laid end to end along the dimension named above; an argument that names none is the same for every part. Nothing has to cross between parts.
All inputs are finite; a program needn't handle non-finite values.
Results may differ from a plain program's by a relative error of at most 0.00025.
Values sent between devices are 32-bit elements; how exact they have to be, the bound alone decides.
A program may use at most 64 MiB of HBM per device.

v0:
```python
import jax
import jax.numpy as jnp
from jax import lax
from jax.experimental import pallas as pl
from jax.experimental.pallas import tpu as pltpu
from jax.sharding import PartitionSpec as P

aspect = 2.0
face_weight = (1.0 / (aspect * aspect), 1.0, 1.0)
mass_factor = (aspect * aspect, 1.0, 1.0)
stiff_weight = (
    2.0 * (face_weight[1] + face_weight[2]),
    2.0 * (face_weight[0] + face_weight[2]),
    2.0 * (face_weight[0] + face_weight[1]),
)
edge_damping = 0.6
shift_ratio = 0.0001
shift_added = 0.05
coarse_along = 0.5625
coarse_across = 0.1875


def extended(block, sides, width):
    for axis, dim in sides:
        count = lax.axis_size(axis)
        forward = [(i, i + 1) for i in range(count - 1)]
        backward = [(target, source) for source, target in forward]
        low = lax.ppermute(
            lax.slice_in_dim(block, block.shape[dim] - width, None, axis=dim), axis, forward
        )
        high = lax.ppermute(lax.slice_in_dim(block, 0, width, axis=dim), axis, backward)
        block = jnp.concatenate([low, block, high], axis=dim)
    return block


def shifted(values, axis_index):
    axis_index = axis_index % values.ndim
    length = values.shape[axis_index]
    widths = [(0, 0)] * values.ndim
    widths[axis_index] = (1, 0)
    return lax.slice_in_dim(jnp.pad(values, widths), 0, length, axis=axis_index)


def spread(per_kind):
    scalar_kind = per_kind[0:1]
    vector_kind = per_kind[1:2]
    return jnp.concatenate([scalar_kind, vector_kind, vector_kind, vector_kind], axis=0)


def edge_coefficients(cell_values, free_edges):
    cells_west = shifted(cell_values, 0)
    cells_south = shifted(cell_values, 1)
    cells_above = shifted(cell_values, 2)
    first_edges = 0.25 * (cell_values + cells_south + cells_above + shifted(cells_above, 1))
    second_edges = 0.25 * (cell_values + cells_west + cells_above + shifted(cells_above, 0))
    third_edges = 0.25 * (cell_values + cells_west + cells_south + shifted(cells_south, 0))
    averages = jnp.stack([first_edges, second_edges, third_edges])
    factors = jnp.array(mass_factor, jnp.float32).reshape(3, 1, 1, 1)
    stiffness = jnp.array(stiff_weight, jnp.float32).reshape(3, 1, 1, 1)
    masses = factors * averages * free_edges
    edge_diagonal = stiffness + masses
    kind_weights = jnp.stack([masses, edge_diagonal * free_edges])
    return (masses, edge_diagonal, kind_weights)


def coarse_weights(kind_weights):
    grouped = kind_weights.reshape(
        kind_weights.shape[:3] + (kind_weights.shape[3] // 2, 2, kind_weights.shape[4] // 2, 2)
    )
    summed = (
        grouped[:, :, :, :, 0, :, 0]
        + grouped[:, :, :, :, 1, :, 0]
        + (grouped[:, :, :, :, 0, :, 1] + grouped[:, :, :, :, 1, :, 1])
    )
    factors = jnp.array([coarse_along, coarse_across, coarse_across], jnp.float32).reshape(
        1, 3, 1, 1, 1
    )
    return summed * factors


def level_from(
    weights_pad, start_east, start_north, start_deep, extent_east, extent_north, extent_deep
):

    def window(component, back_east, back_north, back_deep):
        low_east = start_east - back_east
        low_north = start_north - back_north
        low_deep = start_deep - back_deep
        return weights_pad[
            :,
            component,
            low_east : low_east + extent_east,
            low_north : low_north + extent_north,
            low_deep : low_deep + extent_deep,
        ]

    to_east = window(0, 0, 0, 0)
    to_north = window(1, 0, 0, 0)
    to_deep = window(2, 0, 0, 0)
    to_west = window(0, 1, 0, 0)
    to_south = window(1, 0, 1, 0)
    to_shallow = window(2, 0, 0, 1)
    weight_sum = to_east + to_west + to_north + to_south + to_deep + to_shallow
    return (
        to_east,
        to_north,
        to_deep,
        to_west,
        to_south,
        to_shallow,
        (1.0 + shift_ratio) * weight_sum + shift_added,
    )


def curl_apply(padded, masses):
    extent_east = padded.shape[2] - 2
    extent_north = padded.shape[3] - 2
    extent_deep = padded.shape[4] - 2

    def region(values, move_east, move_north, move_deep, extra_cells):
        return values[
            :,
            move_east : move_east + extent_east + extra_cells,
            move_north : move_north + extent_north + extra_cells,
            move_deep : move_deep + extent_deep + extra_cells,
        ]

    field_east = padded[:, 0]
    field_north = padded[:, 1]
    field_deep = padded[:, 2]
    flux_east = face_weight[0] * (
        region(field_deep, 0, 1, 0, 1)
        - region(field_deep, 0, 0, 0, 1)
        - (region(field_north, 0, 0, 1, 1) - region(field_north, 0, 0, 0, 1))
    )
    flux_north = face_weight[1] * (
        region(field_east, 0, 0, 1, 1)
        - region(field_east, 0, 0, 0, 1)
        - (region(field_deep, 1, 0, 0, 1) - region(field_deep, 0, 0, 0, 1))
    )
    flux_deep = face_weight[2] * (
        region(field_north, 1, 0, 0, 1)
        - region(field_north, 0, 0, 0, 1)
        - (region(field_east, 0, 1, 0, 1) - region(field_east, 0, 0, 0, 1))
    )
    out_east = (
        region(flux_north, 1, 1, 0, 0)
        - region(flux_north, 1, 1, 1, 0)
        - (region(flux_deep, 1, 0, 1, 0) - region(flux_deep, 1, 1, 1, 0))
        + masses[0] * region(field_east, 1, 1, 1, 0)
    )
    out_north = (
        region(flux_deep, 0, 1, 1, 0)
        - region(flux_deep, 1, 1, 1, 0)
        - (region(flux_east, 1, 1, 0, 0) - region(flux_east, 1, 1, 1, 0))
        + masses[1] * region(field_north, 1, 1, 1, 0)
    )
    out_deep = (
        region(flux_east, 1, 0, 1, 0)
        - region(flux_east, 1, 1, 1, 0)
        - (region(flux_north, 0, 1, 1, 0) - region(flux_north, 1, 1, 1, 0))
        + masses[2] * region(field_deep, 1, 1, 1, 0)
    )
    return jnp.stack([out_east, out_north, out_deep], axis=1)


def side_padded(plane_pad, grid_level):
    return (
        spread(grid_level[1]) * plane_pad[..., 2:, 1:-1]
        + spread(grid_level[4]) * plane_pad[..., :-2, 1:-1]
        + spread(grid_level[2]) * plane_pad[..., 1:-1, 2:]
        + spread(grid_level[5]) * plane_pad[..., 1:-1, :-2]
    )


def apply_padded(padded, grid_level):
    center = padded[:, :, 1:-1, 1:-1, 1:-1]
    along_line = (
        spread(grid_level[0]) * padded[:, :, 2:, 1:-1, 1:-1]
        + spread(grid_level[3]) * padded[:, :, :-2, 1:-1, 1:-1]
    )
    return spread(grid_level[6]) * center - (
        along_line + side_padded(padded[:, :, 1:-1], grid_level)
    )


def gradient_adjoint(padded):
    interior = padded[:, :, 1:-1, 1:-1, 1:-1]
    from_west = padded[:, 0, :-2, 1:-1, 1:-1]
    from_south = padded[:, 1, 1:-1, :-2, 1:-1]
    from_above = padded[:, 2, 1:-1, 1:-1, :-2]
    total_flow = (
        from_west - interior[:, 0] + (from_south - interior[:, 1]) + (from_above - interior[:, 2])
    )
    return total_flow[:, None]


def average_adjoint(padded):
    interior = padded[:, :, 1:-1, 1:-1, 1:-1]
    return jnp.stack(
        [
            0.5 * (interior[:, 0] + padded[:, 0, :-2, 1:-1, 1:-1]),
            0.5 * (interior[:, 1] + padded[:, 1, 1:-1, :-2, 1:-1]),
            0.5 * (interior[:, 2] + padded[:, 2, 1:-1, 1:-1, :-2]),
        ],
        axis=1,
    )


def gradient_edges(padded):
    interior = padded[:, 0, 1:-1, 1:-1, 1:-1]
    return jnp.stack(
        [
            padded[:, 0, 2:, 1:-1, 1:-1] - interior,
            padded[:, 0, 1:-1, 2:, 1:-1] - interior,
            padded[:, 0, 1:-1, 1:-1, 2:] - interior,
        ],
        axis=1,
    )


def average_edges(padded):
    return jnp.stack(
        [
            0.5 * (padded[:, 1, 1:-1, 1:-1, 1:-1] + padded[:, 1, 2:, 1:-1, 1:-1]),
            0.5 * (padded[:, 2, 1:-1, 1:-1, 1:-1] + padded[:, 2, 1:-1, 2:, 1:-1]),
            0.5 * (padded[:, 3, 1:-1, 1:-1, 1:-1] + padded[:, 3, 1:-1, 1:-1, 2:]),
        ],
        axis=1,
    )


def restrict_plane(padded):
    extent_north = padded.shape[3] - 2
    extent_deep = padded.shape[4] - 2
    halved = padded[:, :, :, 1 : extent_north + 1 : 2] + 0.5 * (
        padded[:, :, :, 0:extent_north:2] + padded[:, :, :, 2 : extent_north + 2 : 2]
    )
    return halved[..., 1 : extent_deep + 1 : 2] + 0.5 * (
        halved[..., 0:extent_deep:2] + halved[..., 2 : extent_deep + 2 : 2]
    )


def prolong_plane(padded):
    extent_north = padded.shape[3] - 2
    extent_deep = padded.shape[4] - 2
    even_rows = padded[:, :, :, 1 : extent_north + 1]
    odd_rows = 0.5 * (even_rows + padded[:, :, :, 2 : extent_north + 2])
    widened = jnp.stack([even_rows, odd_rows], axis=4)
    widened = widened.reshape(widened.shape[:3] + (2 * extent_north, extent_deep + 2))
    even_layers = widened[..., 1 : extent_deep + 1]
    odd_layers = 0.5 * (even_layers + widened[..., 2 : extent_deep + 2])
    joined = jnp.stack([even_layers, odd_layers], axis=5)
    return joined.reshape(joined.shape[:4] + (2 * extent_deep,))


def factor_lines(below_diagonal, main_diagonal, above_diagonal, entering):

    def forward(factor_before, row_items):
        below_row, main_row, above_row = row_items
        pivots = main_row - below_row * factor_before
        factor = above_row / pivots
        return (factor, (pivots, factor))

    ignored, (pivot_rows, factor_rows) = lax.scan(
        forward,
        entering,
        (
            jnp.moveaxis(below_diagonal, 1, 0),
            jnp.moveaxis(main_diagonal, 1, 0),
            jnp.moveaxis(above_diagonal, 1, 0),
        ),
    )
    return (jnp.moveaxis(pivot_rows, 0, 1), jnp.moveaxis(factor_rows, 0, 1))


def eliminate_rows(source, below_diagonal, pivots):

    def forward(earlier_row, row_items):
        below_row, pivot_row, source_row = row_items
        eliminated = (source_row - spread(below_row) * earlier_row) / spread(pivot_row)
        return (eliminated, eliminated)

    ignored, rows_out = lax.scan(
        forward,
        jnp.zeros(source[:, :, 0].shape, jnp.float32),
        (
            jnp.moveaxis(below_diagonal, 1, 0),
            jnp.moveaxis(pivots, 1, 0),
            jnp.moveaxis(source, 2, 0),
        ),
    )
    return jnp.moveaxis(rows_out, 0, 2)


def substitute_rows(eliminated, factors):

    def backward(next_value, row_items):
        factor_row, reduced_row = row_items
        solved = reduced_row - spread(factor_row) * next_value
        return (solved, solved)

    ignored, rows_out = lax.scan(
        backward,
        jnp.zeros(eliminated[:, :, 0].shape, jnp.float32),
        (jnp.moveaxis(factors, 1, 0), jnp.moveaxis(eliminated, 2, 0)),
        reverse=True,
    )
    return jnp.moveaxis(rows_out, 0, 2)


def plain_solve(right_side, below_diagonal, pivots, factors):

    def forward(earlier_row, row_items):
        below_row, pivot_row, source_row = row_items
        eliminated = (source_row - below_row * earlier_row) / pivot_row
        return (eliminated, eliminated)

    ignored, rows_out = lax.scan(
        forward,
        jnp.zeros(right_side[:, 0].shape, jnp.float32),
        (
            jnp.moveaxis(below_diagonal, 1, 0),
            jnp.moveaxis(pivots, 1, 0),
            jnp.moveaxis(right_side, 1, 0),
        ),
    )

    def backward(next_value, row_items):
        factor_row, reduced_row = row_items
        solved = reduced_row - factor_row * next_value
        return (solved, solved)

    ignored, solved_rows = lax.scan(
        backward,
        jnp.zeros(right_side[:, 0].shape, jnp.float32),
        (jnp.moveaxis(factors, 1, 0), rows_out),
        reverse=True,
    )
    return jnp.moveaxis(solved_rows, 0, 1)


def spike_level(grid_level):
    below_diagonal = -grid_level[3]
    main_diagonal = grid_level[6]
    above_diagonal = -grid_level[0]
    pivots, factors = factor_lines(
        below_diagonal,
        main_diagonal,
        above_diagonal,
        jnp.zeros(main_diagonal[:, 0].shape, jnp.float32),
    )
    inner_zero = jnp.zeros_like(main_diagonal[:, 1:])
    spike_before = plain_solve(
        jnp.concatenate([below_diagonal[:, :1], inner_zero], axis=1),
        below_diagonal,
        pivots,
        factors,
    )
    spike_after = plain_solve(
        jnp.concatenate([inner_zero, above_diagonal[:, -1:]], axis=1),
        below_diagonal,
        pivots,
        factors,
    )
    end_rows = jnp.stack(
        [spike_before[:, 0], spike_before[:, -1], spike_after[:, 0], spike_after[:, -1]], axis=1
    )
    return (
        (below_diagonal, pivots, factors, spike_before, spike_after),
        end_rows.reshape(end_rows.shape[:2] + (1, -1)),
    )


def reduce_chain(coefficients):
    before_first, before_last, after_first, after_last = (
        coefficients[:, member] for member in range(4)
    )

    def forward(beta_before, row_items):
        first_row, last_row, next_first, next_last = row_items
        denominator = 1.0 - first_row * beta_before
        scaled = next_first / denominator
        beta_after = next_last + last_row * beta_before * scaled
        return (beta_after, (denominator, scaled, beta_before, beta_after))

    ignored, outputs = lax.scan(
        forward,
        jnp.zeros(before_first[:, 0].shape, jnp.float32),
        tuple(
            (
                jnp.moveaxis(values, 1, 0)
                for values in (before_first, before_last, after_first, after_last)
            )
        ),
    )
    denominators, scaled_rows, betas_before, betas_after = (
        jnp.moveaxis(values, 0, 1) for values in outputs
    )
    return (before_first, before_last, denominators, scaled_rows, betas_before, betas_after)


def reduced_factors(fine_level, coarse_level):
    fine_data, fine_ends = spike_level(fine_level)
    coarse_data, coarse_ends = spike_level(coarse_level)
    fine_rows, coarse_rows = (
        lax.all_to_all(fine_ends, "gx", split_axis=3, concat_axis=2, tiled=True),
        lax.all_to_all(coarse_ends, "gx", split_axis=3, concat_axis=2, tiled=True),
    )
    return (fine_data + (reduce_chain(fine_rows),), coarse_data + (reduce_chain(coarse_rows),))


def reduced_solve(source, line_data):
    below_diagonal, pivots, factors, spike_before, spike_after, reduced = line_data
    local_rows = substitute_rows(eliminate_rows(source, below_diagonal, pivots), factors)
    end_values = jnp.stack([local_rows[:, :, 0], local_rows[:, :, -1]], axis=2)
    end_values = end_values.reshape(end_values.shape[:3] + (-1,))
    spread_rows = tuple((jnp.moveaxis(spread(values), 1, 0) for values in reduced))
    exchanged = lax.all_to_all(end_values, "gx", split_axis=3, concat_axis=2, tiled=True)
    paired = exchanged.reshape(
        exchanged.shape[:2] + (exchanged.shape[2] // 2, 2, exchanged.shape[3])
    )
    first_values = jnp.moveaxis(paired[:, :, :, 0], 2, 0)
    last_values = jnp.moveaxis(paired[:, :, :, 1], 2, 0)
    before_first, before_last, denominators, scaled_rows, betas_before, betas_after = spread_rows

    def forward(carried, row_items):
        first_row, last_row, couple_first, couple_last, denominator, beta_before = row_items
        leading = (first_row - couple_first * carried) / denominator
        trailing = last_row - couple_last * (carried - beta_before * leading)
        return (trailing, (leading, trailing))

    ignored, (leading_rows, trailing_rows) = lax.scan(
        forward,
        jnp.zeros(first_values[0].shape, jnp.float32),
        (first_values, last_values, before_first, before_last, denominators, betas_before),
    )

    def backward(next_first, row_items):
        leading, trailing, scaled, beta_after = row_items
        solved_first = leading - scaled * next_first
        solved_last = trailing - beta_after * next_first
        return (solved_first, (next_first, solved_last))

    ignored, (next_firsts, solved_lasts) = lax.scan(
        backward,
        jnp.zeros(first_values[0].shape, jnp.float32),
        (leading_rows, trailing_rows, scaled_rows, betas_after),
        reverse=True,
    )
    previous_lasts = jnp.concatenate([jnp.zeros_like(solved_lasts[:1]), solved_lasts[:-1]], axis=0)
    coupled = jnp.stack([previous_lasts, next_firsts], axis=1)
    coupled = jnp.moveaxis(coupled.reshape((-1,) + coupled.shape[2:]), 0, 2)
    couplings = lax.all_to_all(coupled, "gx", split_axis=2, concat_axis=3, tiled=True)
    couplings = couplings.reshape(couplings.shape[:3] + local_rows.shape[3:])
    return (
        local_rows
        - spread(spike_before) * couplings[:, :, 0:1]
        - spread(spike_after) * couplings[:, :, 1:2]
    )


def line_relax(source, line_data):
    return reduced_solve(source, line_data)


def edge_rims(values, rim_width):
    return extended(values, (("gx", 2), ("gy", 3), ("gz", 4)), rim_width)


def node_rims(values):
    return extended(values, (("gx", 2), ("gy", 3), ("gz", 4)), 1)


def coarse_plane(values):
    return node_rims(values)[:, :, 1:-1]


def cycle_body(nodal_source, fine_level, coarse_level, fine_lines, coarse_lines):
    smoothed = line_relax(nodal_source, fine_lines)
    residue = nodal_source - apply_padded(node_rims(smoothed), fine_level)
    coarse_source = restrict_plane(node_rims(residue)[:, :, 1:-1])
    correction = line_relax(coarse_source, coarse_lines)
    correction = line_relax(
        coarse_source + side_padded(coarse_plane(correction), coarse_level), coarse_lines
    )
    widened = coarse_plane(correction)
    smoothed = smoothed + prolong_plane(widened)
    return line_relax(
        nodal_source + side_padded(node_rims(smoothed)[:, :, 1:-1], fine_level), fine_lines
    )


def per_device_permutes(residual, classes, edge_mask, class_weight):
    labels = jnp.arange(class_weight.shape[0], dtype=jnp.int32).reshape(-1, 1, 1, 1)
    cell_values = jnp.sum(
        jnp.where(classes[None] == labels, class_weight.reshape(-1, 1, 1, 1), 0.0), axis=0
    )
    free_edges = (1 - edge_mask).astype(jnp.float32)
    material = jnp.concatenate([cell_values[None], free_edges], axis=0)[None]
    material_pad = edge_rims(material, 2)[0]
    masses_pad, diagonal_pad, kinds_pad = edge_coefficients(material_pad[0], material_pad[1:])
    masses = masses_pad[:, 2:-2, 2:-2, 2:-2]
    edge_diagonal = diagonal_pad[:, 2:-2, 2:-2, 2:-2]
    extent_east = residual.shape[2]
    extent_north = residual.shape[3]
    extent_deep = residual.shape[4]
    fine_level = level_from(kinds_pad, 2, 2, 2, extent_east, extent_north, extent_deep)
    coarse_level = level_from(
        coarse_weights(kinds_pad), 2, 1, 1, extent_east, extent_north // 2, extent_deep // 2
    )
    fine_lines, coarse_lines = reduced_factors(fine_level, coarse_level)
    source = residual * free_edges
    first = edge_damping * source / edge_diagonal * free_edges
    remainder = source - curl_apply(edge_rims(first, 1), masses) * free_edges
    rimmed = node_rims(remainder)
    nodal_source = jnp.concatenate([gradient_adjoint(rimmed), average_adjoint(rimmed)], axis=1)
    potential = cycle_body(nodal_source, fine_level, coarse_level, fine_lines, coarse_lines)
    rimmed = node_rims(potential)
    second = first + (gradient_edges(rimmed) + average_edges(rimmed)) * free_edges
    remainder = source - curl_apply(edge_rims(second, 1), masses) * free_edges
    return second + edge_damping * remainder / edge_diagonal * free_edges


def split_dot(left, right):
    high = left.astype(jnp.bfloat16)
    low = (left - high.astype(jnp.float32)).astype(jnp.bfloat16)
    return jnp.dot(high, right, preferred_element_type=jnp.float32) + jnp.dot(
        low, right, preferred_element_type=jnp.float32
    )


def dot_split(left, right):
    high = right.astype(jnp.bfloat16)
    low = (right - high.astype(jnp.float32)).astype(jnp.bfloat16)
    return jnp.dot(left, high, preferred_element_type=jnp.float32) + jnp.dot(
        left, low, preferred_element_type=jnp.float32
    )


def gather_kernel(
    counts, residual, classes, edge_mask, class_weight, out,
    data, mass, stiff, damp, field, nodal, sides, diagonal, inverse, east_scaled, west_scaled,
    potential, residue, coarse_weight, coarse_sides, coarse_inverse, coarse_east, coarse_west,
    coarse_source, correction, second, result, arrived,
    send_z, recv_z, send_x, recv_x, send_c, recv_c, send_out, recv_out,
):
    ngx, ngy, ngz = counts
    gx, gy, gz = (lax.axis_index(name) for name in ("gx", "gy", "gz"))
    xb, yb, zb = classes.shape
    nx, ny, nz = xb * ngx, yb * ngy, zb * ngz
    yc, zc = ny // 2, nz // 2

    barrier = pltpu.get_barrier_semaphore()
    peers = (
        [{"gx": lax.rem(gx + step, ngx)} for step in range(1, ngx)]
        + [{"gy": lax.rem(gy + step, ngy)} for step in range(1, ngy)]
        + [{"gz": lax.rem(gz + step, ngz)} for step in range(1, ngz)]
    )
    for peer in peers:
        pl.semaphore_signal(barrier, inc=1, device_id=peer, device_id_type=pl.DeviceIdType.MESH)

    def block(low, size, bx, by, bz):
        return data.at[
            pl.ds(low, size),
            pl.ds(bx * xb + 1, xb),
            pl.ds(pl.multiple_of(by * yb, 8), yb),
            pl.ds(pl.multiple_of(bz * zb, 128), zb),
        ]

    own = block(0, 10, gx, gy, gz)
    labels = classes[...]
    cells = jnp.full(labels.shape, class_weight[0], jnp.float32)
    for label in range(1, class_weight.shape[0]):
        cells = jnp.where(labels == label, class_weight[label], cells)
    own[0:3] = residual[0]
    own[3] = cells
    own[4:7] = (1 - edge_mask[...]).astype(jnp.float32)
    own[7:10] = residual[1]

    pl.semaphore_wait(barrier, len(peers))

    sends = []

    def send(source, target_peer, send_sem, recv_sem):
        copy = pltpu.make_async_remote_copy(
            src_ref=source, dst_ref=source, send_sem=send_sem, recv_sem=recv_sem,
            device_id=target_peer, device_id_type=pl.DeviceIdType.MESH,
        )
        copy.start()
        sends.append(copy)

    def arrival(ref, sem_send, sem_recv, peer):
        pltpu.make_async_remote_copy(
            src_ref=ref, dst_ref=ref, send_sem=sem_send, recv_sem=sem_recv,
            device_id=peer, device_id_type=pl.DeviceIdType.MESH,
        ).wait_recv()

    steps = sorted(range(1, ngx), key=lambda step: min(step, ngx - step))

    def to_cores(ky, k, bx, by):
        for kz in range(1, ngz):
            other = lax.rem(gz + ngz - kz, ngz)
            send(block(3 * other, 7, bx, by, gz), {"gz": other}, send_c.at[kz - 1, ky, k], recv_c.at[kz - 1, ky, k])

    def to_rows(k, bx):
        for ky in range(1, ngy):
            send(block(0, 10, bx, gy, gz), {"gy": lax.rem(gy + ngy - ky, ngy)}, send_x.at[ky - 1, k], recv_x.at[ky - 1, k])

    for k in steps:
        send(own, {"gx": lax.rem(gx + ngx - k, ngx)}, send_z.at[k], recv_z.at[k])
    to_rows(0, gx)
    to_cores(0, 0, gx, gy)

    zero_plane = jnp.zeros((ny, nz), jnp.float32)
    for member in range(3, 7):
        data[member, 0] = zero_plane
        data[member, nx + 1] = zero_plane
    for member in range(3):
        field[member, 0] = zero_plane
        field[member, nx + 1] = zero_plane
    for member in range(4):
        for plane in (0, nx + 1, nx + 2):
            potential[member, plane] = zero_plane

    for k in steps:
        bx = lax.rem(gx + k, ngx)
        arrival(block(0, 10, bx, gy, gz), send_z.at[k], recv_z.at[k], {"gx": bx})
        to_rows(k, bx)
        to_cores(0, k, bx, gy)
    for ky in range(1, ngy):
        by = lax.rem(gy + ky, ngy)
        for k in [0] + steps:
            bx = lax.rem(gx + k, ngx)
            arrival(block(0, 10, bx, by, gz), send_x.at[ky - 1, k], recv_x.at[ky - 1, k], {"gy": by})
            to_cores(ky, k, bx, by)
    for kz in range(1, ngz):
        bz = lax.rem(gz + kz, ngz)
        for ky in range(ngy):
            by = lax.rem(gy + ky, ngy)
            for k in [0] + steps:
                bx = lax.rem(gx + k, ngx)
                arrival(block(3 * gz, 7, bx, by, bz), send_c.at[kz - 1, ky, k], recv_c.at[kz - 1, ky, k], {"gz": bz})
    for copy in sends:
        copy.wait_send()

    mine = 7 * gz

    def edges_of(rows, layers):
        at_row = lax.broadcasted_iota(jnp.int32, (rows, layers), 0)
        at_layer = lax.broadcasted_iota(jnp.int32, (rows, layers), 1)
        masks = (at_row == 0, at_row == rows - 1, at_layer == 0, at_layer == layers - 1)

        def y_low(v):
            return jnp.where(masks[0], 0.0, pltpu.roll(v, 1, 0))

        def y_high(v):
            return jnp.where(masks[1], 0.0, pltpu.roll(v, rows - 1, 0))

        def z_low(v):
            return jnp.where(masks[2], 0.0, pltpu.roll(v, 1, 1))

        def z_high(v):
            return jnp.where(masks[3], 0.0, pltpu.roll(v, layers - 1, 1))

        return masks, y_low, y_high, z_low, z_high

    masks, y_low, y_high, z_low, z_high = edges_of(ny, nz)
    _, cy_low, cy_high, cz_low, cz_high = edges_of(yc, zc)

    def level_plane(kind, i, w1, w2, w3, carry, low_y, low_z, sides_ref, inverse_ref, east_ref, west_ref):
        west, east_before = carry
        south = low_y(w2)
        shallow = low_z(w3)
        main = (1.0 + shift_ratio) * (((((w1 + west) + w2) + south) + w3) + shallow) + shift_added
        q = 1.0 / (main - west * east_before)
        east = w1 * q
        sides_ref[kind, 0, i] = w2
        sides_ref[kind, 1, i] = south
        sides_ref[kind, 2, i] = w3
        sides_ref[kind, 3, i] = shallow
        inverse_ref[kind, i] = q
        east_ref[kind, i] = east
        west_ref[kind, i] = west * q
        return (w1, east)

    def materials(i, carry):
        c0 = data[3, i + 1]
        west = data[3, i]
        above = z_low(c0)
        south = y_low(c0)
        both = c0 + west
        averages = (
            0.25 * (((c0 + south) + above) + y_low(above)),
            0.25 * ((both + above) + z_low(west)),
            0.25 * ((both + south) + y_low(west)),
        )
        masses, strong = [], []
        for d in range(3):
            free = data[4 + d, i + 1]
            m = mass_factor[d] * averages[d] * free
            diag = stiff_weight[d] + m
            k = edge_damping * free / diag
            masses.append(m)
            strong.append(diag * free)
            mass[d, i] = m
            stiff[d, i] = strong[d]
            damp[d, i] = k
            field[d, i + 1] = data[mine + d, i + 1] * k
        return (
            level_plane(0, i, *masses, carry[0], y_low, z_low, sides, inverse, east_scaled, west_scaled),
            level_plane(1, i, *strong, carry[1], y_low, z_low, sides, inverse, east_scaled, west_scaled),
        )

    lax.fori_loop(0, nx, materials, ((zero_plane, zero_plane), (zero_plane, zero_plane)))

    def mat(shape, fn):
        return jnp.where(
            fn(lax.broadcasted_iota(jnp.int32, shape, 0), lax.broadcasted_iota(jnp.int32, shape, 1)), 1.0, 0.0
        )

    sum_z = mat((nz, zc), lambda r, c: r // 2 == c).astype(jnp.bfloat16)
    sum_y = mat((nx * yc, nx * ny), lambda r, c: r == c // 2).astype(jnp.bfloat16)
    rest_z = (
        mat((nz, zc), lambda r, c: r == 2 * c)
        + 0.5 * mat((nz, zc), lambda r, c: (r == 2 * c + 1) | (r == 2 * c - 1))
    ).astype(jnp.bfloat16)
    rest_y = (
        mat((nx * yc, nx * ny), lambda r, c: c == 2 * r)
        + 0.5 * mat(
            (nx * yc, nx * ny),
            lambda r, c: (c == 2 * r + 1) | ((c == 2 * r - 1) & (lax.rem(r, yc) != 0)),
        )
    ).astype(jnp.bfloat16)
    prol_z = (
        mat((zc, nz), lambda r, c: c == 2 * r)
        + 0.5 * mat((zc, nz), lambda r, c: (c == 2 * r + 1) | (c == 2 * r - 1))
    ).astype(jnp.bfloat16)
    prol_y = (
        mat((nx * ny, nx * yc), lambda r, c: r == 2 * c)
        + 0.5 * mat(
            (nx * ny, nx * yc),
            lambda r, c: (r == 2 * c + 1) | ((r == 2 * c - 1) & (lax.rem(c, yc) != 0)),
        )
    ).astype(jnp.bfloat16)

    for kind, weights in enumerate((mass, stiff)):
        for d in range(3):
            summed = dot_split(sum_y, split_dot(weights[d].reshape(nx * ny, nz), sum_z))
            factor = coarse_along if d == 0 else coarse_across
            coarse_weight[kind, d] = (factor * summed).reshape(nx, yc, zc)

    def coarse_level(i, carry):
        return tuple(
            level_plane(
                kind, i, coarse_weight[kind, 0, i], coarse_weight[kind, 1, i], coarse_weight[kind, 2, i],
                carry[kind], cy_low, cz_low, coarse_sides, coarse_inverse, coarse_east, coarse_west,
            )
            for kind in range(2)
        )

    coarse_zero = jnp.zeros((yc, zc), jnp.float32)
    lax.fori_loop(0, nx, coarse_level, ((coarse_zero, coarse_zero), (coarse_zero, coarse_zero)))

    def curl_plane(e, m, before):
        (e1, e2, e3), (next2, next3), (b2_before, b3_before) = e, m[0], before
        b1 = face_weight[0] * ((y_high(e3) - e3) - (z_high(e2) - e2))
        b2 = face_weight[1] * ((z_high(e1) - e1) - (next3 - e3))
        b3 = face_weight[2] * ((next2 - e2) - (y_high(e1) - e1))
        b1_y = jnp.where(masks[0], face_weight[0] * e3, pltpu.roll(b1, 1, 0))
        b1_z = jnp.where(masks[2], -face_weight[0] * e2, pltpu.roll(b1, 1, 1))
        b2_z = jnp.where(masks[2], face_weight[1] * e1, pltpu.roll(b2, 1, 1))
        b3_y = jnp.where(masks[0], -face_weight[2] * e1, pltpu.roll(b3, 1, 0))
        m1, m2, m3 = m[1]
        a1 = ((b2_z - b2) - (b3_y - b3)) + m1 * e1
        a2 = ((b3_before - b3) - (b1_z - b1)) + m2 * e2
        a3 = ((b1_y - b1) - (b2_before - b2)) + m3 * e3
        return (a1, a2, a3), (b2, b3)

    def faces_before(e1, e2, e3, next2, next3):
        b2 = face_weight[1] * ((z_high(e1) - e1) - (next3 - e3))
        b3 = face_weight[2] * ((next2 - e2) - (y_high(e1) - e1))
        return (b2, b3)

    def front(i, carry):
        before, rem1_before = carry
        e = tuple(field[d, i + 1] for d in range(3))
        applied, faces = curl_plane(
            e, ((field[1, i + 2], field[2, i + 2]), tuple(mass[d, i] for d in range(3))), before
        )
        r1, r2, r3 = (
            (data[mine + d, i + 1] - applied[d]) * data[4 + d, i + 1] for d in range(3)
        )
        r2_low = y_low(r2)
        r3_low = z_low(r3)
        nodal[0, i] = ((rem1_before - r1) + (r2_low - r2)) + (r3_low - r3)
        nodal[1, i] = 0.5 * (r1 + rem1_before)
        nodal[2, i] = 0.5 * (r2 + r2_low)
        nodal[3, i] = 0.5 * (r3 + r3_low)
        return (faces, r1)

    lax.fori_loop(
        0, nx, front,
        (faces_before(zero_plane, zero_plane, zero_plane, field[1, 1], field[2, 1]), zero_plane),
    )

    def side_sum(refs, kind, i, v, shifts):
        low_y, high_y, low_z, high_z = shifts
        return ((refs[kind, 0, i] * high_y(v) + refs[kind, 1, i] * low_y(v)) + refs[kind, 2, i] * high_z(v)) + refs[
            kind, 3, i
        ] * low_z(v)

    fine_shifts = (y_low, y_high, z_low, z_high)
    coarse_shifts = (cy_low, cy_high, cz_low, cz_high)

    def forward(i, carry):
        done = []
        for member in range(4):
            kind = min(member, 1)
            v = nodal[member, i] * inverse[kind, i] + west_scaled[kind, i] * carry[member]
            potential[member, i + 1] = v
            done.append(v)
        return tuple(done)

    def backward_residue(step, carry):
        i = nx - 1 - step
        done = []
        for member in range(4):
            kind = min(member, 1)
            v = potential[member, i + 1] + east_scaled[kind, i] * carry[member]
            potential[member, i + 1] = v
            residue[member, i] = side_sum(sides, kind, i, v, fine_shifts)
            done.append(v)
        return tuple(done)

    zeros4 = (zero_plane,) * 4
    lax.fori_loop(0, nx, forward, zeros4)
    lax.fori_loop(0, nx, backward_residue, zeros4)

    for member in range(4):
        coarse_source[member] = dot_split(
            rest_y, split_dot(residue[member].reshape(nx * ny, nz), rest_z)
        ).reshape(nx, yc, zc)

    def coarse_solve(first_time):
        def ahead(i, carry):
            done = []
            for member in range(4):
                kind = min(member, 1)
                b = coarse_source[member, i]
                if not first_time:
                    b = b + side_sum(coarse_sides, kind, i, correction[member, i], coarse_shifts)
                v = b * coarse_inverse[kind, i] + coarse_west[kind, i] * carry[member]
                correction[member, i] = v
                done.append(v)
            return tuple(done)

        def back(step, carry):
            i = nx - 1 - step
            done = []
            for member in range(4):
                v = correction[member, i] + coarse_east[min(member, 1), i] * carry[member]
                correction[member, i] = v
                done.append(v)
            return tuple(done)

        lax.fori_loop(0, nx, ahead, (coarse_zero,) * 4)
        lax.fori_loop(0, nx, back, (coarse_zero,) * 4)

    coarse_solve(True)
    for repeat in range(1):
        coarse_solve(False)

    for member in range(4):
        residue[member] = split_dot(
            dot_split(prol_y, correction[member].reshape(nx * yc, zc)), prol_z
        ).reshape(nx, ny, nz)

    def forward_again(i, carry):
        done = []
        for member in range(4):
            kind = min(member, 1)
            smoothed = potential[member, i + 1] + residue[member, i]
            b = nodal[member, i] + side_sum(sides, kind, i, smoothed, fine_shifts)
            v = b * inverse[kind, i] + west_scaled[kind, i] * carry[member]
            potential[member, i + 1] = v
            done.append(v)
        return tuple(done)

    def backward(step, carry):
        i = nx - 1 - step
        done = []
        for member in range(4):
            v = potential[member, i + 1] + east_scaled[min(member, 1), i] * carry[member]
            potential[member, i + 1] = v
            done.append(v)
        return tuple(done)

    lax.fori_loop(0, nx, forward_again, zeros4)
    lax.fori_loop(0, nx, backward, zeros4)

    base = gx * xb

    def update(step, carry):
        at = base + step
        p0, p1, p2, p3 = (potential[member, at] for member in range(4))
        second[0, step] = field[0, at] + ((potential[0, at + 1] - p0) + 0.5 * (p1 + potential[1, at + 1])) * data[4, at]
        second[1, step] = field[1, at] + ((y_high(p0) - p0) + 0.5 * (p2 + y_high(p2))) * data[5, at]
        second[2, step] = field[2, at] + ((z_high(p0) - p0) + 0.5 * (p3 + z_high(p3))) * data[6, at]
        return carry

    lax.fori_loop(0, xb + 2, update, 0)

    def finish(i, before):
        e = tuple(second[d, i + 1] for d in range(3))
        at = base + i
        applied, faces = curl_plane(
            e, ((second[1, i + 2], second[2, i + 2]), tuple(mass[d, at] for d in range(3))), before
        )
        for d in range(3):
            result[d, i] = e[d] + damp[d, at] * (data[mine + d, at + 1] - applied[d])
        return faces

    lax.fori_loop(
        0, xb, finish,
        faces_before(second[0, 0], second[1, 0], second[2, 0], second[1, 1], second[2, 1]),
    )

    def part(bz):
        return result.at[:, :, pl.ds(pl.multiple_of(gy * yb, 8), yb), pl.ds(pl.multiple_of(bz * zb, 128), zb)]

    other = 1 - gz
    swap = pltpu.make_async_remote_copy(
        src_ref=part(other), dst_ref=arrived, send_sem=send_out, recv_sem=recv_out,
        device_id={"gz": other}, device_id_type=pl.DeviceIdType.MESH,
    )
    swap.start()
    out[pl.ds(gz, 1)] = part(gz)[...][None]
    swap.wait()
    out[pl.ds(other, 1)] = arrived[...][None]


def per_device(residual, classes, edge_mask, class_weight):
    counts = tuple(lax.axis_size(name) for name in ("gx", "gy", "gz"))
    ngx, ngy, ngz = counts
    xb, yb, zb = classes.shape
    nx, ny, nz = xb * ngx, yb * ngy, zb * ngz
    cells = nx * ny * nz
    aligned = yb % 8 == 0 and zb % 128 == 0 and (ny // 2) % 8 == 0 and (nz // 2) % 128 == 0
    if ngz != 2 or residual.shape[0] != 2 or not aligned or cells * 4 * 80 > 48 * 2**20:
        return per_device_permutes(residual, classes, edge_mask, class_weight)
    yc, zc = ny // 2, nz // 2

    def held(*shape):
        return pltpu.VMEM(shape, jnp.float32)

    dma = pltpu.SemaphoreType.DMA
    vmem = pl.BlockSpec(memory_space=pltpu.VMEM)
    return pl.pallas_call(
        lambda *refs: gather_kernel(counts, *refs),
        out_shape=jax.ShapeDtypeStruct(residual.shape, jnp.float32),
        in_specs=[vmem, vmem, vmem, pl.BlockSpec(memory_space=pltpu.SMEM)],
        out_specs=vmem,
        scratch_shapes=[
            held(10, nx + 2, ny, nz),
            held(3, nx, ny, nz),
            held(3, nx, ny, nz),
            held(3, nx, ny, nz),
            held(3, nx + 2, ny, nz),
            held(4, nx, ny, nz),
            held(2, 4, nx, ny, nz),
            held(1, 1, 8, 128),
            held(2, nx, ny, nz),
            held(2, nx, ny, nz),
            held(2, nx, ny, nz),
            held(4, nx + 3, ny, nz),
            held(4, nx, ny, nz),
            held(2, 3, nx, yc, zc),
            held(2, 4, nx, yc, zc),
            held(2, nx, yc, zc),
            held(2, nx, yc, zc),
            held(2, nx, yc, zc),
            held(4, nx, yc, zc),
            held(4, nx, yc, zc),
            held(3, xb + 2, ny, nz),
            held(3, xb, ny, nz),
            held(3, xb, yb, zb),
            dma((ngx,)), dma((ngx,)),
            dma((max(ngy - 1, 1), ngx)), dma((max(ngy - 1, 1), ngx)),
            dma((ngz - 1, ngy, ngx)), dma((ngz - 1, ngy, ngx)),
            dma, dma,
        ],
        compiler_params=pltpu.CompilerParams(
            collective_id=0, has_side_effects=True, vmem_limit_bytes=60 * 2**20
        ),
    )(residual, classes, edge_mask, class_weight)


def solution(mesh):
    return jax.shard_map(
        per_device,
        mesh=mesh,
        in_specs=(
            P("period", None, "gx", "gy", "gz"),
            P("gx", "gy", "gz"),
            P(None, "gx", "gy", "gz"),
            P("period"),
        ),
        out_specs=P("period", None, "gx", "gy", "gz"),
        check_vma=False,
    )
```

profile of v0, /device:TPU:0, one launch (start us, length us, event | category | flops | bytes accessed | tf_op | source)
XLA Modules:
  0.0 46.7 jit_solution(10126986559378752911)
XLA Ops:
  0.0 45.1 %shard_map.46 = f32[2,3,4,8,128]{4,3,2,1,0:T(8,128)} custom-call(f32[2,3,4,8,128]{4,3,2,1,0:T(8,128)} %refs_0_.1, s32[4,8,128]{2,1,0:T(8,128)} %refs_1_.1, s32[3,4,8,128]{3,2,1,0:T(8,128)} %refs_2_.1, f32[16]{0:T(128)} %refs_3_.1), custom_call_target="tpu_custom_call" | custom-call | tf_op jit(solution)/shard_map/pallas_call | solution.py:959
  45.1 1.5 %copy.6 = f32[2,3,4,8,128]{4,3,2,1,0:T(8,128)} copy(f32[2,3,4,8,128]{4,3,2,1,0:T(8,128)} %shard_map.46) | data formatting | bytes 196608
where the time goes:
time: 46.8 us; the launch traced here: 46.7 us
  Pallas kernels  45.1 us (96%)
  local copies, waits for them, and re-layouts  1.54 us (3%)
    pallas_call x1, Pallas kernels, per_device(): pl.pallas_call(lambda *refs: gather_kernel(counts, *refs), out_shape=jax....  45.1 us
    unnamed x1, local copies, waits for them, and re-layouts  1.54 us

commit v1 on v0

--- a/solution.py
+++ b/solution.py
@@ -538,6 +538,13 @@
     )
 
 
+UNROLL = 16
+
+
+def looped(low, high, body, carry):
+    return lax.fori_loop(low, high, body, carry, unroll=UNROLL if (high - low) % UNROLL == 0 else True)
+
+
 def gather_kernel(
     counts, residual, classes, edge_mask, class_weight, out,
     data, mass, stiff, damp, field, nodal, sides, diagonal, inverse, east_scaled, west_scaled,
@@ -552,13 +559,17 @@
     yc, zc = ny // 2, nz // 2
 
     barrier = pltpu.get_barrier_semaphore()
-    peers = (
-        [{"gx": lax.rem(gx + step, ngx)} for step in range(1, ngx)]
-        + [{"gy": lax.rem(gy + step, ngy)} for step in range(1, ngy)]
-        + [{"gz": lax.rem(gz + step, ngz)} for step in range(1, ngz)]
-    )
-    for peer in peers:
+    across = {"gy": 1 - gy}
+    partner = {"gz": 1 - gz}
+    sides_of = ((gx > 0, gx - 1, -1), (gx < ngx - 1, gx + 1, 1))
+
+    def signal(peer):
         pl.semaphore_signal(barrier, inc=1, device_id=peer, device_id_type=pl.DeviceIdType.MESH)
+
+    for there, near, _ in sides_of:
+        pl.when(there)(lambda near=near: signal({"gx": near}))
+    signal(across)
+    signal(partner)
 
     def block(low, size, bx, by, bz):
         return data.at[
@@ -573,47 +584,69 @@
     cells = jnp.full(labels.shape, class_weight[0], jnp.float32)
     for label in range(1, class_weight.shape[0]):
         cells = jnp.where(labels == label, class_weight[label], cells)
-    own[0:3] = residual[0]
-    own[3] = cells
-    own[4:7] = (1 - edge_mask[...]).astype(jnp.float32)
+    own[0] = cells
+    own[1:4] = (1 - edge_mask[...]).astype(jnp.float32)
+    own[4:7] = residual[0]
     own[7:10] = residual[1]
 
-    pl.semaphore_wait(barrier, len(peers))
-
-    sends = []
-
-    def send(source, target_peer, send_sem, recv_sem):
-        copy = pltpu.make_async_remote_copy(
-            src_ref=source, dst_ref=source, send_sem=send_sem, recv_sem=recv_sem,
-            device_id=target_peer, device_id_type=pl.DeviceIdType.MESH,
-        )
-        copy.start()
-        sends.append(copy)
-
-    def arrival(ref, sem_send, sem_recv, peer):
-        pltpu.make_async_remote_copy(
-            src_ref=ref, dst_ref=ref, send_sem=sem_send, recv_sem=sem_recv,
+    pl.semaphore_wait(barrier, 2 + (gx + ngx - 1) // ngx + (2 * ngx - 2 - gx) // ngx)
+
+    ranges = ((0, 4), (4, 6), (0, 4))
+    sent = []
+
+    def copy_of(ref, peer, send_sem, recv_sem):
+        return pltpu.make_async_remote_copy(
+            src_ref=ref, dst_ref=ref, send_sem=send_sem, recv_sem=recv_sem,
             device_id=peer, device_id_type=pl.DeviceIdType.MESH,
-        ).wait_recv()
-
-    steps = sorted(range(1, ngx), key=lambda step: min(step, ngx - step))
-
-    def to_cores(ky, k, bx, by):
-        for kz in range(1, ngz):
-            other = lax.rem(gz + ngz - kz, ngz)
-            send(block(3 * other, 7, bx, by, gz), {"gz": other}, send_c.at[kz - 1, ky, k], recv_c.at[kz - 1, ky, k])
-
-    def to_rows(k, bx):
-        for ky in range(1, ngy):
-            send(block(0, 10, bx, gy, gz), {"gy": lax.rem(gy + ngy - ky, ngy)}, send_x.at[ky - 1, k], recv_x.at[ky - 1, k])
-
-    for k in steps:
-        send(own, {"gx": lax.rem(gx + ngx - k, ngx)}, send_z.at[k], recv_z.at[k])
-    to_rows(0, gx)
-    to_cores(0, 0, gx, gy)
+        )
+
+    def along(kind, side, far, bx, by):
+        there, near, _ = sides_of[1 - side]
+        copy = copy_of(block(*ranges[kind], bx, by, gz), {"gx": near}, send_z.at[kind, side, far], recv_z.at[kind, side, far])
+        return there, copy
+
+    def slot(side, far):
+        return 0 if far == 0 else 1 + side * (ngx - 1) + far - 1
+
+    def cross(kind, side, far, bx):
+        at = slot(side, far)
+        return copy_of(block(*ranges[kind], bx, gy, gz), across, send_x.at[kind, at], recv_x.at[kind, at])
+
+    def inner(kind, side, far, bx, by, row, outward):
+        at = slot(side, far)
+        low, size = (0, 4) if kind == 0 else (4 + 3 * ((1 - gz) if outward else gz), 3)
+        return copy_of(
+            block(low, size, bx, by, (gz if outward else 1 - gz)), partner, send_c.at[kind, row, at], recv_c.at[kind, row, at]
+        )
+
+    def start(copy, conditions):
+        run = copy.start
+        for condition in conditions:
+            run = (lambda condition, run: lambda: pl.when(condition)(lambda: run() and None))(condition, run)
+        run()
+        sent.append((conditions, copy))
+
+    def wait_recv(copy, condition):
+        if condition is None:
+            copy.wait_recv()
+        else:
+            pl.when(condition)(lambda: copy.wait_recv())
+
+    def here(side, far):
+        return gx >= far if side == 0 else gx + far < ngx
+
+    def bx_of(side, far):
+        return jnp.maximum(gx - far, 0) if side == 0 else jnp.minimum(gx + far, ngx - 1)
+
+    for kind in range(2):
+        for side in range(2):
+            there, copy = along(kind, side, 0, gx, gy)
+            start(copy, [there])
+        start(cross(kind, 0, 0, gx), [])
+        start(inner(kind, 0, 0, gx, gy, 0, True), [])
 
     zero_plane = jnp.zeros((ny, nz), jnp.float32)
-    for member in range(3, 7):
+    for member in range(4):
         data[member, 0] = zero_plane
         data[member, nx + 1] = zero_plane
     for member in range(3):
@@ -623,28 +656,64 @@
         for plane in (0, nx + 1, nx + 2):
             potential[member, plane] = zero_plane
 
-    for k in steps:
-        bx = lax.rem(gx + k, ngx)
-        arrival(block(0, 10, bx, gy, gz), send_z.at[k], recv_z.at[k], {"gx": bx})
-        to_rows(k, bx)
-        to_cores(0, k, bx, gy)
-    for ky in range(1, ngy):
-        by = lax.rem(gy + ky, ngy)
-        for k in [0] + steps:
-            bx = lax.rem(gx + k, ngx)
-            arrival(block(0, 10, bx, by, gz), send_x.at[ky - 1, k], recv_x.at[ky - 1, k], {"gy": by})
-            to_cores(ky, k, bx, by)
-    for kz in range(1, ngz):
-        bz = lax.rem(gz + kz, ngz)
-        for ky in range(ngy):
-            by = lax.rem(gy + ky, ngy)
-            for k in [0] + steps:
-                bx = lax.rem(gx + k, ngx)
-                arrival(block(3 * gz, 7, bx, by, bz), send_c.at[kz - 1, ky, k], recv_c.at[kz - 1, ky, k], {"gz": bz})
-    for copy in sends:
-        copy.wait_send()
-
-    mine = 7 * gz
+    def z_arrival(kind, side, far, by):
+        bx = bx_of(side, far)
+        return copy_of(
+            block(*ranges[kind], bx, by, gz), partner, send_z.at[kind, side, far - 1], recv_z.at[kind, side, far - 1]
+        )
+
+    for far in range(1, ngx):
+        for kind in range(2):
+            for side in range(2):
+                bx = bx_of(side, far)
+                seen = here(side, far)
+                wait_recv(z_arrival(kind, side, far, gy), seen)
+                if far < ngx - 1:
+                    there, copy = along(kind, side, far, bx, gy)
+                    start(copy, [seen, there])
+                if kind == 1 or far > 1:
+                    start(cross(kind, side, far, bx), [seen])
+                start(inner(kind, side, far, bx, gy, 0, True), [seen])
+            if far == 1 and kind == 0:
+                copy = copy_of(block(0, 4, gx, 1 - gy, gz), across, send_x.at[0, 0], recv_x.at[0, 0])
+                copy.wait_recv()
+                for side in range(2):
+                    there, copy = along(2, side, 0, gx, 1 - gy)
+                    start(copy, [there])
+                start(inner(0, 0, 0, gx, 1 - gy, 1, True), [])
+
+    def x_arrival(kind, side, far):
+        at = slot(side, far)
+        return copy_of(
+            block(*ranges[kind], bx_of(side, far), 1 - gy, gz), across, send_x.at[kind, at], recv_x.at[kind, at]
+        )
+
+    def take_row(kind, side, far):
+        seen = here(side, far) if far else None
+        if kind == 0 and far == 1:
+            wait_recv(z_arrival(2, side, 1, 1 - gy), seen)
+        else:
+            wait_recv(x_arrival(kind, side, far), seen)
+        start(inner(kind, side, far, bx_of(side, far), 1 - gy, 1, True), [seen] if far else [])
+
+    def take_inner(kind):
+        for row in range(2):
+            by = gy if row == 0 else 1 - gy
+            for side, far in [(0, 0)] + [(side, far) for far in range(1, ngx) for side in range(2)]:
+                copy = inner(kind, side, far, bx_of(side, far), by, row, False)
+                wait_recv(copy, here(side, far) if far else None)
+
+    for side in range(2):
+        take_row(0, side, 1)
+    take_row(1, 0, 0)
+    for side in range(2):
+        take_row(1, side, 1)
+    for far in range(2, ngx):
+        for side in range(2):
+            take_row(0, side, far)
+    take_inner(0)
+
+    mine = 4 + 3 * gz
 
     def edges_of(rows, layers):
         at_row = lax.broadcasted_iota(jnp.int32, (rows, layers), 0)
@@ -685,8 +754,8 @@
         return (w1, east)
 
     def materials(i, carry):
-        c0 = data[3, i + 1]
-        west = data[3, i]
+        c0 = data[0, i + 1]
+        west = data[0, i]
         above = z_low(c0)
         south = y_low(c0)
         both = c0 + west
@@ -697,7 +766,7 @@
         )
         masses, strong = [], []
         for d in range(3):
-            free = data[4 + d, i + 1]
+            free = data[1 + d, i + 1]
             m = mass_factor[d] * averages[d] * free
             diag = stiff_weight[d] + m
             k = edge_damping * free / diag
@@ -706,13 +775,16 @@
             mass[d, i] = m
             stiff[d, i] = strong[d]
             damp[d, i] = k
-            field[d, i + 1] = data[mine + d, i + 1] * k
         return (
             level_plane(0, i, *masses, carry[0], y_low, z_low, sides, inverse, east_scaled, west_scaled),
             level_plane(1, i, *strong, carry[1], y_low, z_low, sides, inverse, east_scaled, west_scaled),
         )
 
-    lax.fori_loop(0, nx, materials, ((zero_plane, zero_plane), (zero_plane, zero_plane)))
+    looped(0, nx, materials, ((zero_plane, zero_plane), (zero_plane, zero_plane)))
+
+    for far in range(2, ngx):
+        for side in range(2):
+            take_row(1, side, far)
 
     def mat(shape, fn):
         return jnp.where(
@@ -760,7 +832,16 @@
         )
 
     coarse_zero = jnp.zeros((yc, zc), jnp.float32)
-    lax.fori_loop(0, nx, coarse_level, ((coarse_zero, coarse_zero), (coarse_zero, coarse_zero)))
+    looped(0, nx, coarse_level, ((coarse_zero, coarse_zero), (coarse_zero, coarse_zero)))
+
+    take_inner(1)
+
+    def scale(i, carry):
+        for d in range(3):
+            field[d, i + 1] = data[mine + d, i + 1] * damp[d, i]
+        return carry
+
+    looped(0, nx, scale, 0)
 
     def curl_plane(e, m, before):
         (e1, e2, e3), (next2, next3), (b2_before, b3_before) = e, m[0], before
@@ -789,7 +870,7 @@
             e, ((field[1, i + 2], field[2, i + 2]), tuple(mass[d, i] for d in range(3))), before
         )
         r1, r2, r3 = (
-            (data[mine + d, i + 1] - applied[d]) * data[4 + d, i + 1] for d in range(3)
+            (data[mine + d, i + 1] - applied[d]) * data[1 + d, i + 1] for d in range(3)
         )
         r2_low = y_low(r2)
         r3_low = z_low(r3)
@@ -799,7 +880,7 @@
         nodal[3, i] = 0.5 * (r3 + r3_low)
         return (faces, r1)
 
-    lax.fori_loop(
+    looped(
         0, nx, front,
         (faces_before(zero_plane, zero_plane, zero_plane, field[1, 1], field[2, 1]), zero_plane),
     )
@@ -834,8 +915,8 @@
         return tuple(done)
 
     zeros4 = (zero_plane,) * 4
-    lax.fori_loop(0, nx, forward, zeros4)
-    lax.fori_loop(0, nx, backward_residue, zeros4)
+    looped(0, nx, forward, zeros4)
+    looped(0, nx, backward_residue, zeros4)
 
     for member in range(4):
         coarse_source[member] = dot_split(
@@ -864,8 +945,8 @@
                 done.append(v)
             return tuple(done)
 
-        lax.fori_loop(0, nx, ahead, (coarse_zero,) * 4)
-        lax.fori_loop(0, nx, back, (coarse_zero,) * 4)
+        looped(0, nx, ahead, (coarse_zero,) * 4)
+        looped(0, nx, back, (coarse_zero,) * 4)
 
     coarse_solve(True)
     for repeat in range(1):
@@ -896,20 +977,20 @@
             done.append(v)
         return tuple(done)
 
-    lax.fori_loop(0, nx, forward_again, zeros4)
-    lax.fori_loop(0, nx, backward, zeros4)
+    looped(0, nx, forward_again, zeros4)
+    looped(0, nx, backward, zeros4)
 
     base = gx * xb
 
     def update(step, carry):
         at = base + step
         p0, p1, p2, p3 = (potential[member, at] for member in range(4))
-        second[0, step] = field[0, at] + ((potential[0, at + 1] - p0) + 0.5 * (p1 + potential[1, at + 1])) * data[4, at]
-        second[1, step] = field[1, at] + ((y_high(p0) - p0) + 0.5 * (p2 + y_high(p2))) * data[5, at]
-        second[2, step] = field[2, at] + ((z_high(p0) - p0) + 0.5 * (p3 + z_high(p3))) * data[6, at]
+        second[0, step] = field[0, at] + ((potential[0, at + 1] - p0) + 0.5 * (p1 + potential[1, at + 1])) * data[1, at]
+        second[1, step] = field[1, at] + ((y_high(p0) - p0) + 0.5 * (p2 + y_high(p2))) * data[2, at]
+        second[2, step] = field[2, at] + ((z_high(p0) - p0) + 0.5 * (p3 + z_high(p3))) * data[3, at]
         return carry
 
-    lax.fori_loop(0, xb + 2, update, 0)
+    looped(0, xb + 2, update, 0)
 
     def finish(i, before):
         e = tuple(second[d, i + 1] for d in range(3))
@@ -921,7 +1002,7 @@
             result[d, i] = e[d] + damp[d, at] * (data[mine + d, at + 1] - applied[d])
         return faces
 
-    lax.fori_loop(
+    looped(
         0, xb, finish,
         faces_before(second[0, 0], second[1, 0], second[2, 0], second[1, 1], second[2, 1]),
     )
@@ -937,6 +1018,11 @@
     swap.start()
     out[pl.ds(gz, 1)] = part(gz)[...][None]
     swap.wait()
+    for conditions, copy in sent:
+        finish_send = copy.wait_send
+        for condition in conditions:
+            finish_send = (lambda condition, run: lambda: pl.when(condition)(lambda: run() and None))(condition, finish_send)
+        finish_send()
     out[pl.ds(other, 1)] = arrived[...][None]
 
 
@@ -947,7 +1033,7 @@
     nx, ny, nz = xb * ngx, yb * ngy, zb * ngz
     cells = nx * ny * nz
     aligned = yb % 8 == 0 and zb % 128 == 0 and (ny // 2) % 8 == 0 and (nz // 2) % 128 == 0
-    if ngz != 2 or residual.shape[0] != 2 or not aligned or cells * 4 * 80 > 48 * 2**20:
+    if ngz != 2 or ngy != 2 or residual.shape[0] != 2 or not aligned or cells * 4 * 80 > 48 * 2**20:
         return per_device_permutes(residual, classes, edge_mask, class_weight)
     yc, zc = ny // 2, nz // 2
 
@@ -985,9 +1071,9 @@
             held(3, xb + 2, ny, nz),
             held(3, xb, ny, nz),
             held(3, xb, yb, zb),
-            dma((ngx,)), dma((ngx,)),
-            dma((max(ngy - 1, 1), ngx)), dma((max(ngy - 1, 1), ngx)),
-            dma((ngz - 1, ngy, ngx)), dma((ngz - 1, ngy, ngx)),
+            dma((3, 2, ngx)), dma((3, 2, ngx)),
+            dma((2, 2 * ngx)), dma((2, 2 * ngx)),
+            dma((2, 2, 2 * ngx)), dma((2, 2, 2 * ngx)),
             dma, dma,
         ],
         compiler_params=pltpu.CompilerParams(

time: 46.8 us -> 32.9 us (0.70)
  Pallas kernels: 45.1 us -> 31.2 us
    pallas_call x1, Pallas kernels: 45.1 us -> 31.2 us  [per_device(): pl.pallas_call(lambda *refs: gather_kernel(counts, *refs), out_shape=jax....]
where the time goes in v1:
time: 32.9 us; the launch traced here: 32.7 us
  Pallas kernels  31.2 us (95%)
  local copies, waits for them, and re-layouts  1.54 us (5%)
    pallas_call x1, Pallas kernels, per_device(): pl.pallas_call(lambda *refs: gather_kernel(counts, *refs), out_shape=jax....  31.2 us
    unnamed x1, local copies, waits for them, and re-layouts  1.54 us

profile of v1, /device:TPU:0, one launch (start us, length us, event | category | flops | bytes accessed | tf_op | source)
XLA Modules:
  0.0 32.7 jit_solution(525829195719833505)
XLA Ops:
  0.0 31.2 %shard_map.46 = f32[2,3,4,8,128]{4,3,2,1,0:T(8,128)} custom-call(f32[2,3,4,8,128]{4,3,2,1,0:T(8,128)} %refs_0_.1, s32[4,8,128]{2,1,0:T(8,128)} %refs_1_.1, s32[3,4,8,128]{3,2,1,0:T(8,128)} %refs_2_.1, f32[16]{0:T(128)} %refs_3_.1), custom_call_target="tpu_custom_call" | custom-call | tf_op jit(solution)/shard_map/pallas_call | solution.py:1045
  31.2 1.5 %copy.6 = f32[2,3,4,8,128]{4,3,2,1,0:T(8,128)} copy(f32[2,3,4,8,128]{4,3,2,1,0:T(8,128)} %shard_map.46) | data formatting | bytes 196608

commit v2 on v1

--- a/solution.py
+++ b/solution.py
@@ -571,10 +571,13 @@
     signal(across)
     signal(partner)
 
-    def block(low, size, bx, by, bz):
+    half = xb // 2 if xb % 2 == 0 else xb
+    pieces = xb // half
+
+    def block(low, size, bx, by, bz, piece=None):
         return data.at[
             pl.ds(low, size),
-            pl.ds(bx * xb + 1, xb),
+            pl.ds(bx * xb + 1, xb) if piece is None else pl.ds(bx * xb + 1 + piece * half, half),
             pl.ds(pl.multiple_of(by * yb, 8), yb),
             pl.ds(pl.multiple_of(bz * zb, 128), zb),
         ]
@@ -591,7 +594,7 @@
 
     pl.semaphore_wait(barrier, 2 + (gx + ngx - 1) // ngx + (2 * ngx - 2 - gx) // ngx)
 
-    ranges = ((0, 4), (4, 6), (0, 4))
+    ranges = ((0, 4),) * pieces + ((4, 6),) * pieces
     sent = []
 
     def copy_of(ref, peer, send_sem, recv_sem):
@@ -602,7 +605,7 @@
 
     def along(kind, side, far, bx, by):
         there, near, _ = sides_of[1 - side]
-        copy = copy_of(block(*ranges[kind], bx, by, gz), {"gx": near}, send_z.at[kind, side, far], recv_z.at[kind, side, far])
+        copy = copy_of(block(*ranges[kind], bx, by, gz, kind % pieces), {"gx": near}, send_z.at[kind, side, far], recv_z.at[kind, side, far])
         return there, copy
 
     def slot(side, far):
@@ -610,13 +613,13 @@
 
     def cross(kind, side, far, bx):
         at = slot(side, far)
-        return copy_of(block(*ranges[kind], bx, gy, gz), across, send_x.at[kind, at], recv_x.at[kind, at])
+        return copy_of(block(*ranges[kind], bx, gy, gz, kind % pieces), across, send_x.at[kind, at], recv_x.at[kind, at])
 
     def inner(kind, side, far, bx, by, row, outward):
         at = slot(side, far)
-        low, size = (0, 4) if kind == 0 else (4 + 3 * ((1 - gz) if outward else gz), 3)
+        low, size = (0, 4) if kind < pieces else (4 + 3 * ((1 - gz) if outward else gz), 3)
         return copy_of(
-            block(low, size, bx, by, (gz if outward else 1 - gz)), partner, send_c.at[kind, row, at], recv_c.at[kind, row, at]
+            block(low, size, bx, by, (gz if outward else 1 - gz), kind % pieces), partner, send_c.at[kind, row, at], recv_c.at[kind, row, at]
         )
 
     def start(copy, conditions):
@@ -638,7 +641,7 @@
     def bx_of(side, far):
         return jnp.maximum(gx - far, 0) if side == 0 else jnp.minimum(gx + far, ngx - 1)
 
-    for kind in range(2):
+    for kind in range(2 * pieces):
         for side in range(2):
             there, copy = along(kind, side, 0, gx, gy)
             start(copy, [there])
@@ -659,11 +662,22 @@
     def z_arrival(kind, side, far, by):
         bx = bx_of(side, far)
         return copy_of(
-            block(*ranges[kind], bx, by, gz), partner, send_z.at[kind, side, far - 1], recv_z.at[kind, side, far - 1]
-        )
+            block(*ranges[kind], bx, by, gz, kind % pieces), partner, send_z.at[kind, side, far - 1], recv_z.at[kind, side, far - 1]
+        )
+
+    def x_arrival(kind, side, far):
+        at = slot(side, far)
+        return copy_of(
+            block(*ranges[kind], bx_of(side, far), 1 - gy, gz, kind % pieces), across, send_x.at[kind, at], recv_x.at[kind, at]
+        )
+
+    def take_row(kind, side, far):
+        seen = here(side, far) if far else None
+        wait_recv(x_arrival(kind, side, far), seen)
+        start(inner(kind, side, far, bx_of(side, far), 1 - gy, 1, True), [seen] if far else [])
 
     for far in range(1, ngx):
-        for kind in range(2):
+        for kind in range(2 * pieces):
             for side in range(2):
                 bx = bx_of(side, far)
                 seen = here(side, far)
@@ -671,30 +685,11 @@
                 if far < ngx - 1:
                     there, copy = along(kind, side, far, bx, gy)
                     start(copy, [seen, there])
-                if kind == 1 or far > 1:
+                if True:
                     start(cross(kind, side, far, bx), [seen])
                 start(inner(kind, side, far, bx, gy, 0, True), [seen])
-            if far == 1 and kind == 0:
-                copy = copy_of(block(0, 4, gx, 1 - gy, gz), across, send_x.at[0, 0], recv_x.at[0, 0])
-                copy.wait_recv()
-                for side in range(2):
-                    there, copy = along(2, side, 0, gx, 1 - gy)
-                    start(copy, [there])
-                start(inner(0, 0, 0, gx, 1 - gy, 1, True), [])
-
-    def x_arrival(kind, side, far):
-        at = slot(side, far)
-        return copy_of(
-            block(*ranges[kind], bx_of(side, far), 1 - gy, gz), across, send_x.at[kind, at], recv_x.at[kind, at]
-        )
-
-    def take_row(kind, side, far):
-        seen = here(side, far) if far else None
-        if kind == 0 and far == 1:
-            wait_recv(z_arrival(2, side, 1, 1 - gy), seen)
-        else:
-            wait_recv(x_arrival(kind, side, far), seen)
-        start(inner(kind, side, far, bx_of(side, far), 1 - gy, 1, True), [seen] if far else [])
+            if far == 1:
+                take_row(kind, 0, 0)
 
     def take_inner(kind):
         for row in range(2):
@@ -703,15 +698,12 @@
                 copy = inner(kind, side, far, bx_of(side, far), by, row, False)
                 wait_recv(copy, here(side, far) if far else None)
 
-    for side in range(2):
-        take_row(0, side, 1)
-    take_row(1, 0, 0)
-    for side in range(2):
-        take_row(1, side, 1)
-    for far in range(2, ngx):
-        for side in range(2):
-            take_row(0, side, far)
-    take_inner(0)
+    for far in range(1, ngx):
+        for kind in range(2 * pieces if far == 1 else pieces):
+            for side in range(2):
+                take_row(kind, side, far)
+    for kind in range(pieces):
+        take_inner(kind)
 
     mine = 4 + 3 * gz
 
@@ -783,8 +775,9 @@
     looped(0, nx, materials, ((zero_plane, zero_plane), (zero_plane, zero_plane)))
 
     for far in range(2, ngx):
-        for side in range(2):
-            take_row(1, side, far)
+        for kind in range(pieces, 2 * pieces):
+            for side in range(2):
+                take_row(kind, side, far)
 
     def mat(shape, fn):
         return jnp.where(
@@ -834,7 +827,8 @@
     coarse_zero = jnp.zeros((yc, zc), jnp.float32)
     looped(0, nx, coarse_level, ((coarse_zero, coarse_zero), (coarse_zero, coarse_zero)))
 
-    take_inner(1)
+    for kind in range(pieces, 2 * pieces):
+        take_inner(kind)
 
     def scale(i, carry):
         for d in range(3):
@@ -1071,9 +1065,9 @@
             held(3, xb + 2, ny, nz),
             held(3, xb, ny, nz),
             held(3, xb, yb, zb),
-            dma((3, 2, ngx)), dma((3, 2, ngx)),
-            dma((2, 2 * ngx)), dma((2, 2 * ngx)),
-            dma((2, 2, 2 * ngx)), dma((2, 2, 2 * ngx)),
+            dma((4, 2, ngx)), dma((4, 2, ngx)),
+            dma((4, 2 * ngx)), dma((4, 2 * ngx)),
+            dma((4, 2, 2 * ngx)), dma((4, 2, 2 * ngx)),
             dma, dma,
         ],
         compiler_params=pltpu.CompilerParams(

time: 32.9 us -> 32.3 us (0.982)
  Pallas kernels: 31.2 us -> 30.5 us
    pallas_call x1, Pallas kernels: 31.2 us -> 30.5 us  [per_device(): pl.pallas_call(lambda *refs: gather_kernel(counts, *refs), out_shape=jax....]
where the time goes in v2:
time: 32.3 us; the launch traced here: 32.1 us
  Pallas kernels  30.5 us (94%)
  local copies, waits for them, and re-layouts  1.54 us (5%)
    pallas_call x1, Pallas kernels, per_device(): pl.pallas_call(lambda *refs: gather_kernel(counts, *refs), out_shape=jax....  30.5 us
    unnamed x1, local copies, waits for them, and re-layouts  1.54 us

profile of v2, /device:TPU:0, one launch (start us, length us, event | category | flops | bytes accessed | tf_op | source)
XLA Modules:
  0.0 32.1 jit_solution(5117873660780621660)
XLA Ops:
  0.0 30.5 %shard_map.46 = f32[2,3,4,8,128]{4,3,2,1,0:T(8,128)} custom-call(f32[2,3,4,8,128]{4,3,2,1,0:T(8,128)} %refs_0_.1, s32[4,8,128]{2,1,0:T(8,128)} %refs_1_.1, s32[3,4,8,128]{3,2,1,0:T(8,128)} %refs_2_.1, f32[16]{0:T(128)} %refs_3_.1), custom_call_target="tpu_custom_call" | custom-call | tf_op jit(solution)/shard_map/pallas_call | solution.py:1039
  30.5 1.5 %copy.6 = f32[2,3,4,8,128]{4,3,2,1,0:T(8,128)} copy(f32[2,3,4,8,128]{4,3,2,1,0:T(8,128)} %shard_map.46) | data formatting | bytes 196608
